TPU v7x, 512 devices: a whole 4x8x8 slice. The times are simulated.
512 devices in a mesh: site: 2 (over core), rows: 8 (over z), cols: 32 (over y, x).
Axes of the slice: x: 4, y: 8, z: 8, core: 2. Of those that a mesh axis runs over, the one named last changes fastest.
Arguments:
- tracer: float32 [512, 1024, 128], P(('site', 'rows'), 'cols'), parts along dimension 0, may hold values from 0.5 to 2
- flow_y: float32 [512, 1024, 128], P(('site', 'rows'), 'cols'), parts along dimension 0, may hold values from -0.3 to 0.3
- flow_x: float32 [512, 1024, 128], P(('site', 'rows'), 'cols'), parts along dimension 0, may hold values from -0.3 to 0.3
Outputs:
- scaled_field: float32 [512, 1024, 128], P(('site', 'rows'), 'cols'), parts along dimension 0
- tracer_end: float32 [512, 1024, 128], P(('site', 'rows'), 'cols'), parts along dimension 0
There are 2 independent parts, one for each index of `site`. A program takes and returns all parts, laid end to end along the dimension named above; each array names one. Nothing has to cross between parts.
All inputs are finite; a program needn't handle non-finite values.
Results may differ from a plain program's by a relative error of at most 0.00002.
Values sent between devices are 32-bit elements; how exact they have to be, the bound alone decides.
No kernel may reach another device: no remote copies, remote signals or barrier semaphores. Data moves between devices by JAX's collectives and lax.ppermute only.
A program may use at most 64 MiB of HBM per device.

v0:
```python
import jax
import jax.numpy as jnp
from jax import lax
from jax.sharding import PartitionSpec as P

STEPS = 6


def with_halo(block, sides, width):
    for axis, dim in sides:
        count = lax.axis_size(axis)
        forward = [(i, i + 1) for i in range(count - 1)]
        backward = [(target, source) for source, target in forward]
        low = lax.ppermute(
            lax.slice_in_dim(block, block.shape[dim] - width, None, axis=dim), axis, forward
        )
        high = lax.ppermute(lax.slice_in_dim(block, 0, width, axis=dim), axis, backward)
        block = jnp.concatenate([low, block, high], axis=dim)
    return block


def sent_to_all(shard, axis):
    copies = jnp.broadcast_to(shard, (lax.axis_size(axis), *shard.shape))
    return lax.all_to_all(copies, axis, split_axis=0, concat_axis=0, tiled=True)


def of_everyone(shard, axis):
    everything = sent_to_all(shard, axis)
    return jnp.sum(everything, axis=0)


def in_one(arrays, axis):
    ends = [0]
    for a in arrays:
        ends.append(ends[-1] + a.size)
    running = of_everyone(jnp.concatenate([a.ravel() for a in arrays]), axis)
    return tuple((running[b:e].reshape(a.shape) for a, b, e in zip(arrays, ends, ends[1:])))


def strip_edges(values, dims):
    for dim in dims:
        values = lax.slice_in_dim(values, 1, values.shape[dim] - 1, axis=dim)
    return values


def neighbour(values, dim, start, dims):
    others = [other for other in dims if other != dim]
    values = strip_edges(values, others)
    return lax.slice_in_dim(values, start, start + values.shape[dim] - 2, axis=dim)


def one_step(padded, flow_y, flow_x):
    middle = strip_edges(padded, (0, 1))
    lower = [neighbour(padded, dim, 0, (0, 1)) for dim in (0, 1)]
    upper = [neighbour(padded, dim, 2, (0, 1)) for dim in (0, 1)]
    slopes = [above - below for above, below in zip(upper, lower)]
    smooth_rate = 0.05
    spread = lower[0] + upper[0] + lower[1] + upper[1] - 4.0 * middle
    return middle - flow_y * slopes[0] - flow_x * slopes[1] + smooth_rate * spread


def shards(tracer, flow_y, flow_x):
    padded = with_halo(tracer, (("rows", 0), ("cols", 1)), STEPS)
    wide_parts = with_halo(
        jnp.concatenate([flow_y, flow_x], axis=2), (("rows", 0), ("cols", 1)), STEPS - 1
    )
    wide_flow_y, wide_flow_x = jnp.split(wide_parts, 2, axis=2)
    for step in range(STEPS):
        later = one_step(padded, wide_flow_y, wide_flow_x)
        values = later
        margin = STEPS - 1 - step
        place = lax.axis_index("rows") * tracer.shape[0] - margin + jnp.arange(values.shape[0])
        keep_cells = (place >= 0) & (place < tracer.shape[0] * lax.axis_size("rows"))
        values = jnp.where(keep_cells.reshape((-1,) + (1,) * 2), values, 0.0)
        place = lax.axis_index("cols") * tracer.shape[1] - margin + jnp.arange(values.shape[1])
        keep_cells = (place >= 0) & (place < tracer.shape[1] * lax.axis_size("cols"))
        values = jnp.where(keep_cells.reshape((-1,) + (1,) * 1), values, 0.0)
        later = values
        if step < STEPS - 1:
            wide_flow_y = strip_edges(wide_flow_y, (0, 1))
            wide_flow_x = strip_edges(wide_flow_x, (0, 1))
        padded = later
    tracer = padded
    count = tracer.shape[1] * lax.axis_size("cols")
    guess = 1.0
    moved = tracer - guess
    totals, squares = in_one(
        (jnp.sum(moved, axis=1, keepdims=True), jnp.sum(moved * moved, axis=1, keepdims=True)),
        "cols",
    )
    line_mean = guess + totals / count
    centred = tracer - line_mean
    line_variance = squares / count - totals / count * (totals / count)
    scaled_field = centred * lax.rsqrt(line_variance + 0.0001)
    return (scaled_field, tracer)


def solution(mesh):
    placed = (
        P(("site", "rows"), "cols", None),
        P(("site", "rows"), "cols", None),
        P(("site", "rows"), "cols", None),
    )
    return jax.shard_map(
        shards,
        mesh=mesh,
        in_specs=placed,
        out_specs=(P(("site", "rows"), "cols", None), P(("site", "rows"), "cols", None)),
        check_vma=False,
    )
```

profile of v0, /device:TPU:68, one launch (start us, length us, event | category | flops | bytes accessed | tf_op | source)
XLA Modules:
  0.0 87.9 jit_solution(11635322656763004369)
XLA Ops:
  0.6 1.1 %constant_dynamic-update-slice_fusion.4 = f32[32,32,256]{2,1,0:T(8,128)S(1)} fusion(f32[32,32,128]{2,1,0:T(8,128)} %param.4), kind=kLoop, calls=%fused_computation.56 | loop fusion | bytes 1048576
  1.8 1.1 %constant_dynamic-update-slice_fusion.3 = f32[32,32,256]{2,1,0:T(8,128)S(1)} fusion(f32[32,32,256]{2,1,0:T(8,128)S(1)} %constant_dynamic-update-slice_fusion.4, f32[32,32,128]{2,1,0:T(8,128)} %param.5), kind=kLoop, calls=%fused_computation.55 | loop fusion | bytes 1048576 | tf_op jit(solution)/shard_map/concatenate | solution.py:65
  2.9 1.9 %collective-permute-start.5 = (f32[5,32,256]{2,1,0:T(8,128)S(1)}, f32[5,32,256]{2,1,0:T(8,128)S(1)}, u32[]{:S(2)}, u32[]{:S(2)}) collective-permute-start(f32[5,32,256]{2,1,0:T(8,128)S(1)} %get-tuple-element.8), channel_id=1, source_target_pairs={{32,0},{64,32},{96,64},{128,96},{160,128},{192,160},{224,192},{33,... | collective-permute-start | bytes 491528 | tf_op jit(solution)/shard_map/ppermute | solution.py:17
  4.8 4.3 %collective-permute-start.4 = (f32[5,32,256]{2,1,0:T(8,128)S(1)}, f32[5,32,256]{2,1,0:T(8,128)S(1)}, u32[]{:S(2)}, u32[]{:S(2)}) collective-permute-start(f32[5,32,256]{2,1,0:T(8,128)S(1)} %get-tuple-element.7), channel_id=1, source_target_pairs={{0,32},{32,64},{64,96},{96,128},{128,160},{160,192},{192,224},{1,3... | collective-permute-start | bytes 491528 | tf_op jit(solution)/shard_map/ppermute | solution.py:14
  9.2 4.3 %collective-permute-start = (f32[6,32,128]{2,1,0:T(8,128)S(1)}, f32[6,32,128]{2,1,0:T(8,128)S(1)}, u32[]{:S(2)}, u32[]{:S(2)}) collective-permute-start(f32[6,32,128]{2,1,0:T(8,128)S(1)} %get-tuple-element.12), channel_id=1, source_target_pairs={{0,32},{32,64},{64,96},{96,128},{128,160},{160,192},{192,224},{1,3... | collective-permute-start | bytes 294920 | tf_op jit(solution)/shard_map/ppermute | solution.py:14
  13.4 1.9 %collective-permute-start.1 = (f32[6,32,128]{2,1,0:T(8,128)S(1)}, f32[6,32,128]{2,1,0:T(8,128)S(1)}, u32[]{:S(2)}, u32[]{:S(2)}) collective-permute-start(f32[6,32,128]{2,1,0:T(8,128)S(1)} %get-tuple-element.11), channel_id=1, source_target_pairs={{32,0},{64,32},{96,64},{128,96},{160,128},{192,160},{224,192},{33,... | collective-permute-start | bytes 294920 | tf_op jit(solution)/shard_map/ppermute | solution.py:17
  15.5 0.2 collective-permute-done
  15.7 5.8 %collective-permute-done.1 = f32[6,32,128]{2,1,0:T(8,128)S(1)} collective-permute-done((f32[6,32,128]{2,1,0:T(8,128)S(1)}, f32[6,32,128]{2,1,0:T(8,128)S(1)}, u32[]{:S(2)}, u32[]{:S(2)}) %collective-permute-start.1) | collective-permute-done | bytes 98336 | tf_op jit(solution)/shard_map/ppermute | solution.py:17
  21.6 2.4 %collective-permute-start.3 = (f32[44,6,128]{2,1,0:T(8,128)S(1)}, f32[44,6,128]{2,1,0:T(8,128)S(1)}, u32[]{:S(2)}, u32[]{:S(2)}) collective-permute-start(f32[44,6,128]{2,1,0:T(8,128)S(1)} %get-tuple-element.10), channel_id=1, source_target_pairs={{1,0},{2,1},{3,2},{4,3},{5,4},{6,5},{7,6},{8,7},{9,8},{10,9},{11,1... | collective-permute-start | bytes 405512 | tf_op jit(solution)/shard_map/ppermute | solution.py:17
  24.0 3.4 %collective-permute-start.2 = (f32[44,6,128]{2,1,0:T(8,128)S(1)}, f32[44,6,128]{2,1,0:T(8,128)S(1)}, u32[]{:S(2)}, u32[]{:S(2)}) collective-permute-start(f32[44,6,128]{2,1,0:T(8,128)S(1)} %get-tuple-element.9), channel_id=1, source_target_pairs={{0,1},{1,2},{2,3},{3,4},{4,5},{5,6},{6,7},{7,8},{8,9},{9,10},{10,1... | collective-permute-start | bytes 405512 | tf_op jit(solution)/shard_map/ppermute | solution.py:14
  27.4 0.1 pad_maximum_fusion.4
  27.5 2.4 %collective-permute-start.7 = (f32[42,5,256]{2,1,0:T(8,128)S(1)}, f32[42,5,256]{2,1,0:T(8,128)S(1)}, u32[]{:S(2)}, u32[]{:S(2)}) collective-permute-start(f32[42,5,256]{2,1,0:T(8,128)S(1)} %get-tuple-element.6), channel_id=1, source_target_pairs={{1,0},{2,1},{3,2},{4,3},{5,4},{6,5},{7,6},{8,7},{9,8},{10,9},{11,1... | collective-permute-start | bytes 645128 | tf_op jit(solution)/shard_map/ppermute | solution.py:17
  30.0 4.7 %collective-permute-start.6 = (f32[42,5,256]{2,1,0:T(8,128)S(1)}, f32[42,5,256]{2,1,0:T(8,128)S(1)}, u32[]{:S(2)}, u32[]{:S(2)}) collective-permute-start(f32[42,5,256]{2,1,0:T(8,128)S(1)} %get-tuple-element.5), channel_id=1, source_target_pairs={{0,1},{1,2},{2,3},{3,4},{4,5},{5,6},{6,7},{7,8},{8,9},{9,10},{10,1... | collective-permute-start | bytes 645128 | tf_op jit(solution)/shard_map/ppermute | solution.py:14
  34.7 0.1 pad_maximum_fusion.1
  34.8 3.9 %collective-permute-done.7 = f32[42,5,256]{2,1,0:T(8,128)S(1)} collective-permute-done((f32[42,5,256]{2,1,0:T(8,128)S(1)}, f32[42,5,256]{2,1,0:T(8,128)S(1)}, u32[]{:S(2)}, u32[]{:S(2)}) %collective-permute-start.7) | collective-permute-done | bytes 215072 | tf_op jit(solution)/shard_map/ppermute | solution.py:17
  38.8 1.2 %collective-permute-done.6 = f32[42,5,256]{2,1,0:T(8,128)S(1)} collective-permute-done((f32[42,5,256]{2,1,0:T(8,128)S(1)}, f32[42,5,256]{2,1,0:T(8,128)S(1)}, u32[]{:S(2)}, u32[]{:S(2)}) %collective-permute-start.6) | collective-permute-done | bytes 215072 | tf_op jit(solution)/shard_map/ppermute | solution.py:14
  40.0 0.3 pad_maximum_fusion
  40.3 0.7 fusion.3
  41.0 0.6 fusion.8
  41.6 0.7 fusion.13
  42.3 0.6 fusion.18
  42.9 0.0 copy-start
  42.9 0.0 copy-start.1
  43.0 0.6 fusion.23
  43.6 0.4 copy-done
  44.0 0.2 copy-done.1
  44.1 0.5 add_reduce_fusion
  44.7 0.0 copy-start.2
  44.7 0.9 %broadcast_in_dim.153 = f32[32,1,8192]{2,1,0:T(1,128)S(1)} broadcast(f32[8192]{0:T(1024)S(1)} %pad_maximum_fusion.5), dimensions={2} | broadcast | bytes 1081344 | tf_op jit(solution)/shard_map/broadcast_in_dim | solution.py:23
  45.6 40.7 %all_to_all.6 = f32[32,1,8192]{2,1,0:T(1,128)S(1)} all-to-all(f32[32,1,8192]{2,1,0:T(1,128)S(1)} %broadcast_in_dim.153), channel_id=1, replica_groups=mesh['site'=2,'rows'=8,'cols'=32] {'cols'}, dimensions={0} | all-to-all | bytes 2097152 | tf_op jit(solution)/shard_map/all_to_all | solution.py:24
  86.3 0.7 reduce_sum.29
  87.0 0.9 subtract_multiply_fusion
  (21 shorter events, 0.2 us)
Async XLA Ops:
  0.6 8.5 %copy-start.3 = (f32[32,32,128]{2,1,0:T(8,128)S(1)}, f32[32,32,128]{2,1,0:T(8,128)}, u32[]{:S(2)}) copy-start(f32[32,32,128]{2,1,0:T(8,128)} %param.3) | copy-start | bytes 1572868
  2.9 24.5 %collective-permute-start.5 = (f32[5,32,256]{2,1,0:T(8,128)S(1)}, f32[5,32,256]{2,1,0:T(8,128)S(1)}, u32[]{:S(2)}, u32[]{:S(2)}) collective-permute-start(f32[5,32,256]{2,1,0:T(8,128)S(1)} %get-tuple-element.8), channel_id=1, source_target_pairs={{32,0},{64,32},{96,64},{128,96},{160,128},{192,160},{224,192},{33,... | collective-permute-start | bytes 491528 | tf_op jit(solution)/shard_map/ppermute | solution.py:17
  4.8 22.6 %collective-permute-start.4 = (f32[5,32,256]{2,1,0:T(8,128)S(1)}, f32[5,32,256]{2,1,0:T(8,128)S(1)}, u32[]{:S(2)}, u32[]{:S(2)}) collective-permute-start(f32[5,32,256]{2,1,0:T(8,128)S(1)} %get-tuple-element.7), channel_id=1, source_target_pairs={{0,32},{32,64},{64,96},{96,128},{128,160},{160,192},{192,224},{1,3... | collective-permute-start | bytes 491528 | tf_op jit(solution)/shard_map/ppermute | solution.py:14
  9.2 6.5 %collective-permute-start = (f32[6,32,128]{2,1,0:T(8,128)S(1)}, f32[6,32,128]{2,1,0:T(8,128)S(1)}, u32[]{:S(2)}, u32[]{:S(2)}) collective-permute-start(f32[6,32,128]{2,1,0:T(8,128)S(1)} %get-tuple-element.12), channel_id=1, source_target_pairs={{0,32},{32,64},{64,96},{96,128},{128,160},{160,192},{192,224},{1,3... | collective-permute-start | bytes 294920 | tf_op jit(solution)/shard_map/ppermute | solution.py:14
  13.4 8.1 %collective-permute-start.1 = (f32[6,32,128]{2,1,0:T(8,128)S(1)}, f32[6,32,128]{2,1,0:T(8,128)S(1)}, u32[]{:S(2)}, u32[]{:S(2)}) collective-permute-start(f32[6,32,128]{2,1,0:T(8,128)S(1)} %get-tuple-element.11), channel_id=1, source_target_pairs={{32,0},{64,32},{96,64},{128,96},{160,128},{192,160},{224,192},{33,... | collective-permute-start | bytes 294920 | tf_op jit(solution)/shard_map/ppermute | solution.py:17
  21.6 13.1 %collective-permute-start.3 = (f32[44,6,128]{2,1,0:T(8,128)S(1)}, f32[44,6,128]{2,1,0:T(8,128)S(1)}, u32[]{:S(2)}, u32[]{:S(2)}) collective-permute-start(f32[44,6,128]{2,1,0:T(8,128)S(1)} %get-tuple-element.10), channel_id=1, source_target_pairs={{1,0},{2,1},{3,2},{4,3},{5,4},{6,5},{7,6},{8,7},{9,8},{10,9},{11,1... | collective-permute-start | bytes 405512 | tf_op jit(solution)/shard_map/ppermute | solution.py:17
  24.0 10.7 %collective-permute-start.2 = (f32[44,6,128]{2,1,0:T(8,128)S(1)}, f32[44,6,128]{2,1,0:T(8,128)S(1)}, u32[]{:S(2)}, u32[]{:S(2)}) collective-permute-start(f32[44,6,128]{2,1,0:T(8,128)S(1)} %get-tuple-element.9), channel_id=1, source_target_pairs={{0,1},{1,2},{2,3},{3,4},{4,5},{5,6},{6,7},{7,8},{8,9},{9,10},{10,1... | collective-permute-start | bytes 405512 | tf_op jit(solution)/shard_map/ppermute | solution.py:14
  27.5 11.3 %collective-permute-start.7 = (f32[42,5,256]{2,1,0:T(8,128)S(1)}, f32[42,5,256]{2,1,0:T(8,128)S(1)}, u32[]{:S(2)}, u32[]{:S(2)}) collective-permute-start(f32[42,5,256]{2,1,0:T(8,128)S(1)} %get-tuple-element.6), channel_id=1, source_target_pairs={{1,0},{2,1},{3,2},{4,3},{5,4},{6,5},{7,6},{8,7},{9,8},{10,9},{11,1... | collective-permute-start | bytes 645128 | tf_op jit(solution)/shard_map/ppermute | solution.py:17
  30.0 10.0 %collective-permute-start.6 = (f32[42,5,256]{2,1,0:T(8,128)S(1)}, f32[42,5,256]{2,1,0:T(8,128)S(1)}, u32[]{:S(2)}, u32[]{:S(2)}) collective-permute-start(f32[42,5,256]{2,1,0:T(8,128)S(1)} %get-tuple-element.5), channel_id=1, source_target_pairs={{0,1},{1,2},{2,3},{3,4},{4,5},{5,6},{6,7},{7,8},{8,9},{9,10},{10,1... | collective-permute-start | bytes 645128 | tf_op jit(solution)/shard_map/ppermute | solution.py:14
  42.9 1.0 %copy-start = (f32[32,32,128]{2,1,0:T(8,128)S(1)}, f32[32,32,128]{2,1,0:T(8,128)}, u32[]{:S(2)}) copy-start(f32[32,32,128]{2,1,0:T(8,128)} %param.5) | copy-start | bytes 1572868
  42.9 1.2 %copy-start.1 = (f32[32,32,128]{2,1,0:T(8,128)S(1)}, f32[32,32,128]{2,1,0:T(8,128)}, u32[]{:S(2)}) copy-start(f32[32,32,128]{2,1,0:T(8,128)} %param.4) | copy-start | bytes 1572868
  44.7 42.4 %copy-start.2 = (f32[32,32,128]{2,1,0:T(8,128)}, f32[32,32,128]{2,1,0:T(8,128)S(1)}, u32[]{:S(2)}) copy-start(f32[32,32,128]{2,1,0:T(8,128)S(1)} %get-tuple-element.4) | copy-start | bytes 1572868
where the time goes:
time: 88.3 us; the launch traced here: 87.9 us
  blocking collectives  40.7 us (46%)
  starting transfers between devices  25.4 us (29%)
  waiting for transfers between devices  11.1 us (13%)
  other arithmetic  5.88 us (7%)
  local copies, waits for them, and re-layouts  3.87 us (4%)
  between operations  0.95 us (1%)
    all_to_all x1, blocking collectives, sent_to_all(): return lax.all_to_all(copies, axis, split_axis=0, concat_axis=0, tiled=True)  40.7 us
    ppermute x4, starting transfers between devices, with_halo(): lax.ppermute(lax.slice_in_dim(block, block.shape[dim] - width, None, axis...  16.7 us
    ppermute x4, waiting for transfers between devices, with_halo(): lax.ppermute(lax.slice_in_dim(block, 0, width, axis=dim), axis, backward)  9.75 us
    ppermute x4, starting transfers between devices, with_halo(): lax.ppermute(lax.slice_in_dim(block, 0, width, axis=dim), axis, backward)  8.73 us
    select_n x5, other arithmetic, shards(): values = jnp.where(keep_cells.reshape((-1,) + (1,) * 1), values, 0.0)  3.2 us
    unnamed x11, local copies, waits for them, and re-layouts  1.78 us
  transfers between devices with their start and end apart: 8, of which 4 were waited for; matrix products, arithmetic and copies ran while one was open for 0% of the time, Pallas kernels for 0%

commit v1 on v0

v1 whole, which is shorter than its diff:
```python
import jax
import jax.numpy as jnp
from jax import lax
from jax.sharding import Mesh, PartitionSpec as P

STEPS = 6
COLS = ("y", "x")


def neighbours(block, axis, dim, low, high):
    count = lax.axis_size(axis) if isinstance(axis, str) else 32
    forward = [(i, i + 1) for i in range(count - 1)]
    backward = [(target, source) for source, target in forward]
    return lax.ppermute(high, axis, forward), lax.ppermute(low, axis, backward)


def sum_over(values, axis):
    count = lax.axis_size(axis)
    copies = jnp.broadcast_to(values, (count, *values.shape))
    return jnp.sum(lax.all_to_all(copies, axis, 0, 0, tiled=True), axis=0)


def strip_edges(values, dims):
    for dim in dims:
        values = lax.slice_in_dim(values, 1, values.shape[dim] - 1, axis=dim)
    return values


def neighbour(values, dim, start, dims):
    others = [other for other in dims if other != dim]
    values = strip_edges(values, others)
    return lax.slice_in_dim(values, start, start + values.shape[dim] - 2, axis=dim)


def one_step(padded, flow_y, flow_x):
    middle = strip_edges(padded, (0, 1))
    lower = [neighbour(padded, dim, 0, (0, 1)) for dim in (0, 1)]
    upper = [neighbour(padded, dim, 2, (0, 1)) for dim in (0, 1)]
    slopes = [above - below for above, below in zip(upper, lower)]
    smooth_rate = 0.05
    spread = lower[0] + upper[0] + lower[1] + upper[1] - 4.0 * middle
    return middle - flow_y * slopes[0] - flow_x * slopes[1] + smooth_rate * spread


def shards(tracer, flow_y, flow_x):
    size = tracer.shape[0]
    width, inner = STEPS, STEPS - 1
    parts = (tracer, flow_y, flow_x)
    widths = (width, inner, inner)
    low = jnp.concatenate([p[:w] for p, w in zip(parts, widths)], axis=0)
    high = jnp.concatenate([p[size - w :] for p, w in zip(parts, widths)], axis=0)
    before, after = neighbours(None, "rows", 0, low, high)
    cuts = ((0, width), (width, width + inner), (width + inner, width + 2 * inner))
    parts = [
        jnp.concatenate([before[b:e], p, after[b:e]], axis=0) for p, (b, e) in zip(parts, cuts)
    ]
    tall = [parts[0]] + [jnp.pad(p, ((1, 1), (0, 0), (0, 0))) for p in parts[1:]]
    low = jnp.concatenate([p[:, :w] for p, w in zip(tall, widths)], axis=1)
    high = jnp.concatenate([p[:, size - w :] for p, w in zip(tall, widths)], axis=1)
    before, after = neighbours(None, COLS, 1, low, high)
    padded = jnp.concatenate([before[:, :width], parts[0], after[:, :width]], axis=1)
    wide_flow_y, wide_flow_x = [
        jnp.concatenate([before[1:-1, b:e], p, after[1:-1, b:e]], axis=1)
        for p, (b, e) in zip(parts[1:], cuts[1:])
    ]
    for step in range(STEPS):
        values = one_step(padded, wide_flow_y, wide_flow_x)
        margin = STEPS - 1 - step
        place = lax.axis_index("rows") * tracer.shape[0] - margin + jnp.arange(values.shape[0])
        keep_cells = (place >= 0) & (place < tracer.shape[0] * lax.axis_size("rows"))
        values = jnp.where(keep_cells.reshape((-1,) + (1,) * 2), values, 0.0)
        place = lax.axis_index(COLS) * tracer.shape[1] - margin + jnp.arange(values.shape[1])
        keep_cells = (place >= 0) & (place < tracer.shape[1] * 32)
        values = jnp.where(keep_cells.reshape((-1,) + (1,) * 1), values, 0.0)
        if step < STEPS - 1:
            wide_flow_y = strip_edges(wide_flow_y, (0, 1))
            wide_flow_x = strip_edges(wide_flow_x, (0, 1))
        padded = values
    tracer = padded
    count = tracer.shape[1] * 32
    guess = 1.0
    moved = tracer - guess
    both = jnp.concatenate([jnp.sum(moved, axis=1), jnp.sum(moved * moved, axis=1)], axis=0)
    both = sum_over(sum_over(both, "x"), "y")
    totals, squares = both[:size, None], both[size:, None]
    line_mean = guess + totals / count
    centred = tracer - line_mean
    line_variance = squares / count - totals / count * (totals / count)
    scaled_field = centred * lax.rsqrt(line_variance + 0.0001)
    return (scaled_field, tracer)


def solution(mesh):
    mesh = Mesh(mesh.devices.reshape(2, 8, 8, 4), ("site", "rows", "y", "x"))
    placed = P(("site", "rows"), COLS, None)
    return jax.shard_map(
        shards, mesh=mesh, in_specs=(placed,) * 3, out_specs=(placed,) * 2, check_vma=False
    )
```

time: 88.3 us -> 70.9 us (0.80)
  the two profiles are of different devices: /device:TPU:68 before, /device:TPU:192 now
where the time goes in v1:
time: 70.9 us; the launch traced here: 70.5 us
  blocking collectives  29.5 us (42%)
  waiting for transfers between devices  17.6 us (25%)
  starting transfers between devices  12.1 us (17%)
  other arithmetic  6.15 us (9%)
  local copies, waits for them, and re-layouts  4.13 us (6%)
  between operations  0.93 us (1%)
    all_to_all x2, blocking collectives, sum_over(): return jnp.sum(lax.all_to_all(copies, axis, 0, 0, tiled=True), axis=0)  29.5 us
    ppermute x2, waiting for transfers between devices, neighbours(): lax.ppermute(low, axis, backward)  9.46 us
    ppermute x2, starting transfers between devices, neighbours(): lax.ppermute(high, axis, forward)  8.91 us
    ppermute x2, waiting for transfers between devices, neighbours(): lax.ppermute(high, axis, forward)  8.18 us
    select_n x5, other arithmetic, shards(): values = jnp.where(keep_cells.reshape((-1,) + (1,) * 1), values, 0.0)  3.47 us
    ppermute x2, starting transfers between devices, neighbours(): lax.ppermute(low, axis, backward)  3.21 us
    slice x2, local copies, waits for them, and re-layouts, shards(): p[size - w:]  2.04 us
    unnamed x12, local copies, waits for them, and re-layouts  1.88 us
  transfers between devices with their start and end apart: 4, of which 4 were waited for; matrix products, arithmetic and copies ran while one was open for 1% of the time, Pallas kernels for 0%

profile of v1, /device:TPU:192, one launch (start us, length us, event | category | flops | bytes accessed | tf_op | source)
XLA Modules:
  0.0 70.5 jit_solution(12222186038809817658)
XLA Ops:
  0.6 1.0 %fusion.31 = (f32[6,32,128]{2,1,0:T(8,128)S(1)}, f32[6,32,128]{2,1,0:T(8,128)S(1)}) fusion(f32[32,32,128]{2,1,0:T(8,128)} %param.3), kind=kLoop, calls=%fused_computation.75 | loop fusion | bytes 393216 | tf_op jit(solution)/shard_map/slice | solution.py:51
  1.6 0.0 copy-start.1
  1.6 1.1 %fusion.32 = (f32[5,32,128]{2,1,0:T(8,128)S(1)}, f32[5,32,128]{2,1,0:T(8,128)S(1)}, f32[5,32,128]{2,1,0:T(8,128)S(1)}, f32[5,32,128]{2,1,0:T(8,128)S(1)}) fusion(f32[32,32,128]{2,1,0:T(8,128)} %param.4, f32[32,32,128]{2,1,0:T(8,128)} %param.5), kind=kLoop, calls=%fused_computation.76 | loop fusion | bytes 655360 | tf_op jit(solution)/shard_map/slice | solution.py:51
  2.7 5.5 %collective-permute-start = (f32[16,32,128]{2,1,0:T(8,128)S(1)}, f32[16,32,128]{2,1,0:T(8,128)S(1)}, u32[]{:S(2)}, u32[]{:S(2)}) collective-permute-start(f32[16,32,128]{2,1,0:T(8,128)S(1)} %pad_maximum_fusion.5), channel_id=1, source_target_pairs={{0,32},{32,64},{64,96},{96,128},{128,160},{160,192},{192,224},{1,3... | collective-permute-start | bytes 786440 | tf_op jit(solution)/shard_map/ppermute | solution.py:14
  8.2 1.9 %collective-permute-start.1 = (f32[16,32,128]{2,1,0:T(8,128)S(1)}, f32[16,32,128]{2,1,0:T(8,128)S(1)}, u32[]{:S(2)}, u32[]{:S(2)}) collective-permute-start(f32[16,32,128]{2,1,0:T(8,128)S(1)} %pad_maximum_fusion.6), channel_id=1, source_target_pairs={{32,0},{64,32},{96,64},{128,96},{160,128},{192,160},{224,192},{33,... | collective-permute-start | bytes 786440 | tf_op jit(solution)/shard_map/ppermute | solution.py:14
  10.2 3.5 %collective-permute-done = f32[16,32,128]{2,1,0:T(8,128)S(1)} collective-permute-done((f32[16,32,128]{2,1,0:T(8,128)S(1)}, f32[16,32,128]{2,1,0:T(8,128)S(1)}, u32[]{:S(2)}, u32[]{:S(2)}) %collective-permute-start) | collective-permute-done | bytes 262176 | tf_op jit(solution)/shard_map/ppermute | solution.py:14
  13.8 5.3 %collective-permute-done.1 = f32[16,32,128]{2,1,0:T(8,128)S(1)} collective-permute-done((f32[16,32,128]{2,1,0:T(8,128)S(1)}, f32[16,32,128]{2,1,0:T(8,128)S(1)}, u32[]{:S(2)}, u32[]{:S(2)}) %collective-permute-start.1) | collective-permute-done | bytes 262176 | tf_op jit(solution)/shard_map/ppermute | solution.py:14
  19.1 0.0 copy-start
  19.1 0.0 copy-done.1
  19.2 0.9 %copy-done = f32[32,32,128]{2,1,0:T(8,128)S(1)} copy-done((f32[32,32,128]{2,1,0:T(8,128)S(1)}, f32[32,32,128]{2,1,0:T(8,128)}, u32[]{:S(2)}) %copy-start) | copy-done | bytes 524312
  20.3 0.9 %copy-done.2 = f32[32,32,128]{2,1,0:T(8,128)S(1)} copy-done((f32[32,32,128]{2,1,0:T(8,128)S(1)}, f32[32,32,128]{2,1,0:T(8,128)}, u32[]{:S(2)}) %copy-start.2) | copy-done | bytes 524312
  21.2 0.1 fusion.24
  21.4 3.4 %collective-permute-start.2 = (f32[44,16,128]{2,1,0:T(8,128)S(1)}, f32[44,16,128]{2,1,0:T(8,128)S(1)}, u32[]{:S(2)}, u32[]{:S(2)}) collective-permute-start(f32[44,16,128]{2,1,0:T(8,128)S(1)} %get-tuple-element.5), channel_id=1, source_target_pairs={{0,1},{1,2},{2,3},{3,4},{4,5},{5,6},{6,7},{7,8},{8,9},{9,10},{10,1... | collective-permute-start | bytes 1081352 | tf_op jit(solution)/shard_map/ppermute | solution.py:14
  24.8 1.3 %collective-permute-start.3 = (f32[44,16,128]{2,1,0:T(8,128)S(1)}, f32[44,16,128]{2,1,0:T(8,128)S(1)}, u32[]{:S(2)}, u32[]{:S(2)}) collective-permute-start(f32[44,16,128]{2,1,0:T(8,128)S(1)} %get-tuple-element.6), channel_id=1, source_target_pairs={{1,0},{2,1},{3,2},{4,3},{5,4},{6,5},{7,6},{8,7},{9,8},{10,9},{11,1... | collective-permute-start | bytes 1081352 | tf_op jit(solution)/shard_map/ppermute | solution.py:14
  26.1 0.5 compare_and_fusion.2
  26.6 4.6 %collective-permute-done.2 = f32[44,16,128]{2,1,0:T(8,128)S(1)} collective-permute-done((f32[44,16,128]{2,1,0:T(8,128)S(1)}, f32[44,16,128]{2,1,0:T(8,128)S(1)}, u32[]{:S(2)}, u32[]{:S(2)}) %collective-permute-start.2) | collective-permute-done | bytes 360480 | tf_op jit(solution)/shard_map/ppermute | solution.py:14
  31.3 4.1 %collective-permute-done.3 = f32[44,16,128]{2,1,0:T(8,128)S(1)} collective-permute-done((f32[44,16,128]{2,1,0:T(8,128)S(1)}, f32[44,16,128]{2,1,0:T(8,128)S(1)}, u32[]{:S(2)}, u32[]{:S(2)}) %collective-permute-start.3) | collective-permute-done | bytes 360480 | tf_op jit(solution)/shard_map/ppermute | solution.py:14
  35.4 0.1 pad_maximum_fusion
  35.7 0.1 pad_maximum_fusion.1
  35.8 0.1 pad_maximum_fusion.2
  35.9 0.0 copy-start.4
  35.9 0.0 copy-start.5
  36.0 0.9 %select_select_fusion = f32[42,42,128]{2,1,0:T(8,128)S(1)} fusion(f32[44,44,128]{2,1,0:T(8,128)S(1)} %pad_maximum_fusion, pred[42]{0:T(512)(128)(4,1)S(1)} %get-tuple-element.29, pred[42]{0:T(512)(128)(4,1)S(1)} %get-tuple-element.30, f32[42,5,128]{2,1,0:T(8,128)S(1)} %get-tuple-element.20, f32[5,32,128]{2,1,0:T(8,128)S(1)} %get-tuple-element.24, ...), kind=kLoop, calls=%fused_computation.5 | loop fusion | flops 5193216 | bytes 7225428 | tf_op jit(solution)/shard_map/jit(_where)/select_n | solution.py:74
  36.9 0.6 fusion.3
  37.6 0.7 fusion.8
  38.2 0.6 fusion.13
  38.9 0.6 fusion.19
  39.5 0.5 add_reduce_fusion
  40.0 0.0 copy-start.3
  40.0 11.9 %all_to_all.10 = f32[4,64,128]{2,1,0:T(8,128)S(1)} all-to-all(f32[4,64,128]{2,1,0:T(8,128)S(1)} %broadcast_in_dim.158), channel_id=1, replica_groups=mesh['site'=2,'rows'=8,'y'=8,'x'=4] {'x'}, dimensions={0} | all-to-all | bytes 262144 | tf_op jit(solution)/shard_map/all_to_all | solution.py:20
  52.0 17.6 %all_to_all.11 = f32[8,64,128]{2,1,0:T(8,128)S(1)} all-to-all(f32[8,64,128]{2,1,0:T(8,128)S(1)} %broadcast_in_dim.159), channel_id=1, replica_groups=mesh['site'=2,'rows'=8,'y'=8,'x'=4] {'y'}, dimensions={0} | all-to-all | bytes 524288 | tf_op jit(solution)/shard_map/all_to_all | solution.py:20
  69.6 0.9 %subtract_multiply_fusion = f32[32,32,128]{2,1,0:T(8,128)} fusion(f32[32,32,128]{2,1,0:T(8,128)S(1)} %get-tuple-element.4, f32[32,128]{1,0:T(8,128)S(1)} %get-tuple-element.26, f32[32,128]{1,0:T(8,128)S(1)} %get-tuple-element.25), kind=kLoop, calls=%fused_computation.39 | loop fusion | flops 262144 | bytes 1081344 | tf_op jit(solution)/shard_map/mul | solution.py:89
  (29 shorter events, 0.4 us)
Async XLA Ops:
  1.6 17.6 %copy-start.1 = (f32[32,32,128]{2,1,0:T(8,128)S(1)}, f32[32,32,128]{2,1,0:T(8,128)}, u32[]{:S(2)}) copy-start(f32[32,32,128]{2,1,0:T(8,128)} %param.4) | copy-start | bytes 1572868
  2.7 11.0 %collective-permute-start = (f32[16,32,128]{2,1,0:T(8,128)S(1)}, f32[16,32,128]{2,1,0:T(8,128)S(1)}, u32[]{:S(2)}, u32[]{:S(2)}) collective-permute-start(f32[16,32,128]{2,1,0:T(8,128)S(1)} %pad_maximum_fusion.5), channel_id=1, source_target_pairs={{0,32},{32,64},{64,96},{96,128},{128,160},{160,192},{192,224},{1,3... | collective-permute-start | bytes 786440 | tf_op jit(solution)/shard_map/ppermute | solution.py:14
  8.2 10.9 %collective-permute-start.1 = (f32[16,32,128]{2,1,0:T(8,128)S(1)}, f32[16,32,128]{2,1,0:T(8,128)S(1)}, u32[]{:S(2)}, u32[]{:S(2)}) collective-permute-start(f32[16,32,128]{2,1,0:T(8,128)S(1)} %pad_maximum_fusion.6), channel_id=1, source_target_pairs={{32,0},{64,32},{96,64},{128,96},{160,128},{192,160},{224,192},{33,... | collective-permute-start | bytes 786440 | tf_op jit(solution)/shard_map/ppermute | solution.py:14
  19.1 1.0 %copy-start = (f32[32,32,128]{2,1,0:T(8,128)S(1)}, f32[32,32,128]{2,1,0:T(8,128)}, u32[]{:S(2)}) copy-start(f32[32,32,128]{2,1,0:T(8,128)} %param.5) | copy-start | bytes 1572868
  20.2 1.0 %copy-start.2 = (f32[32,32,128]{2,1,0:T(8,128)S(1)}, f32[32,32,128]{2,1,0:T(8,128)}, u32[]{:S(2)}) copy-start(f32[32,32,128]{2,1,0:T(8,128)} %param.3) | copy-start | bytes 1572868
  21.4 9.9 %collective-permute-start.2 = (f32[44,16,128]{2,1,0:T(8,128)S(1)}, f32[44,16,128]{2,1,0:T(8,128)S(1)}, u32[]{:S(2)}, u32[]{:S(2)}) collective-permute-start(f32[44,16,128]{2,1,0:T(8,128)S(1)} %get-tuple-element.5), channel_id=1, source_target_pairs={{0,1},{1,2},{2,3},{3,4},{4,5},{5,6},{6,7},{7,8},{8,9},{9,10},{10,1... | collective-permute-start | bytes 1081352 | tf_op jit(solution)/shard_map/ppermute | solution.py:14
  24.8 10.6 %collective-permute-start.3 = (f32[44,16,128]{2,1,0:T(8,128)S(1)}, f32[44,16,128]{2,1,0:T(8,128)S(1)}, u32[]{:S(2)}, u32[]{:S(2)}) collective-permute-start(f32[44,16,128]{2,1,0:T(8,128)S(1)} %get-tuple-element.6), channel_id=1, source_target_pairs={{1,0},{2,1},{3,2},{4,3},{5,4},{6,5},{7,6},{8,7},{9,8},{10,9},{11,1... | collective-permute-start | bytes 1081352 | tf_op jit(solution)/shard_map/ppermute | solution.py:14
  35.9 1.0 %copy-start.4 = (pred[40]{0:T(512)(128)(4,1)S(1)}, pred[40]{0:T(512)(128)(4,1)}, u32[]{:S(2)}) copy-start(pred[40]{0:T(512)(128)(4,1)} %get-tuple-element.31) | copy-start | bytes 124
  35.9 1.0 %copy-start.5 = (pred[40]{0:T(512)(128)(4,1)S(1)}, pred[40]{0:T(512)(128)(4,1)}, u32[]{:S(2)}) copy-start(pred[40]{0:T(512)(128)(4,1)} %get-tuple-element.32) | copy-start | bytes 124
  40.0 30.5 %copy-start.3 = (f32[32,32,128]{2,1,0:T(8,128)}, f32[32,32,128]{2,1,0:T(8,128)S(1)}, u32[]{:S(2)}) copy-start(f32[32,32,128]{2,1,0:T(8,128)S(1)} %get-tuple-element.4) | copy-start | bytes 1572868

commit v2 on v1

v2 whole, which is shorter than its diff:
```python
import functools

import jax
import jax.numpy as jnp
from jax import lax
from jax.experimental import pallas as pl
from jax.experimental.pallas import tpu as pltpu
from jax.sharding import Mesh, PartitionSpec as P

STEPS = 6
SIZE = 32
LANES = 128
ROWS = "rows"
COLS = ("y", "x")
HALO = STEPS
TALL = SIZE + 2 * HALO
WIDE = SIZE + 16
BLOCK = slice(HALO, HALO + SIZE)
CENTRE = slice(8, 8 + SIZE)
WORK = (TALL, WIDE, LANES)
GUESS = 1.0
F32 = jnp.float32
VMEM = pl.BlockSpec(memory_space=pltpu.VMEM)


def size_of(axis):
    sizes = [lax.axis_size(a) for a in ((axis,) if isinstance(axis, str) else axis)]
    return functools.reduce(lambda a, b: a * b, sizes)


def swap_with(block, axis, odd):
    pairs = []
    for low in range(odd, size_of(axis) - 1, 2):
        pairs += [(low, low + 1), (low + 1, low)]
    return lax.ppermute(block, axis, pairs)


def turned(tiles, shift):
    return pltpu.roll(tiles, shift % 8, axis=tiles.ndim - 2)


def pack_kernel(t_in, fy_in, fx_in, t, fy, fx, col_a, col_b, row_a, row_b, sems):
    blocks = ((t_in, t), (fy_in, fy), (fx_in, fx))
    copies = [pltpu.make_async_copy(src, dst, sems.at[k]) for k, (src, dst) in enumerate(blocks)]
    for copy in copies:
        copy.start()
    even_row = lax.axis_index(ROWS) % 2 == 0
    even_col = lax.axis_index(COLS) % 2 == 0
    sub = lax.broadcasted_iota(jnp.int32, (SIZE, 8, LANES), 1)
    for copy in copies:
        copy.wait()
    t_low, fy_low, fx_low = [v[:, 0:8] for v in (t, fy, fx)]
    t_high, fy_high, fx_high = [v[:, SIZE - 8 :] for v in (t, fy, fx)]
    first = (
        jnp.where(sub < 6, t_low, turned(fx_low, 6)),
        jnp.where(sub < 5, fy_low, turned(fx_low, 3)),
    )
    last = (
        jnp.where(sub >= 2, t_high, turned(fx_high, 5)),
        jnp.where(sub >= 3, fy_high, turned(fx_high, 3)),
    )
    for k in range(2):
        col_a[:, 8 * k : 8 * k + 8] = jnp.where(even_col, last[k], first[k])
        col_b[:, 8 * k : 8 * k + 8] = jnp.where(even_col, first[k], last[k])
    for out, top in ((row_a, even_row), (row_b, jnp.logical_not(even_row))):
        out[0:6] = t[pl.ds(jnp.where(top, SIZE - 6, 0), 6)]
        out[6:11] = fy[pl.ds(jnp.where(top, SIZE - 5, 0), 5)]
        out[11:16] = fx[pl.ds(jnp.where(top, SIZE - 5, 0), 5)]


def corner_kernel(col_a, col_b, cor_a, cor_b):
    even_row = lax.axis_index(ROWS) % 2 == 0
    for out, top in ((cor_a, even_row), (cor_b, jnp.logical_not(even_row))):
        at = pl.ds(jnp.where(top, SIZE - STEPS + 1, 0), STEPS - 1)
        out[:, 0:16] = col_a[at]
        out[:, 16:32] = col_b[at]


def sum_kernel(parts, out):
    total = jnp.sum(parts[...], axis=0)
    for k in range(out.shape[0]):
        out[k] = total


def beside(packed, west):
    one, two = packed[:, 0:8], packed[:, 8:16]
    sub = lax.broadcasted_iota(jnp.int32, one.shape, 1)
    if west:
        return one, two, jnp.where(sub < 5, turned(one, 3), turned(two, 5))
    return one, two, jnp.where(sub < 2, turned(one, 2), turned(two, 5))


def steps_kernel(t, fy, fx, col_a, col_b, row_a, row_b, cor_a, cor_b, end, sums, p0, p1, cy, cx):
    for src, dst in ((t, p0), (fy, cy), (fx, cx)):
        dst[BLOCK, CENTRE] = src[...]
    row, col = lax.axis_index(ROWS), lax.axis_index(COLS)
    even_row, even_col = row % 2 == 0, col % 2 == 0
    first_row, last_row = row == 0, row == lax.axis_size(ROWS) - 1
    has_west, has_east = col > 0, col < size_of(COLS) - 1
    west, east = jnp.where(even_col, col_b[...], col_a[...]), jnp.where(even_col, col_a[...], col_b[...])
    south, north = jnp.where(even_row, row_b[...], row_a[...]), jnp.where(even_row, row_a[...], row_b[...])
    cuts = ((0, 6), (6, 11), (11, 16))
    for v, at, is_west in ((west, 0, True), (east, 8 + SIZE, False)):
        for tile, dst in zip(beside(v, is_west), (p0, cy, cx)):
            dst[BLOCK, at : at + 8] = tile
    for (b, e), dst in zip(cuts, (p0, cy, cx)):
        dst[HALO - (e - b) : HALO, CENTRE] = south[b:e]
        dst[HALO + SIZE : HALO + SIZE + e - b, CENTRE] = north[b:e]
    south, north = jnp.where(even_row, cor_b[...], cor_a[...]), jnp.where(even_row, cor_a[...], cor_b[...])
    for v, rows in ((south, slice(1, HALO)), (north, slice(HALO + SIZE, TALL - 1))):
        of_a, of_b = v[:, 0:16], v[:, 16:32]
        for packed, at, is_west in (
            (jnp.where(even_col, of_b, of_a), 0, True),
            (jnp.where(even_col, of_a, of_b), 8 + SIZE, False),
        ):
            for tile, dst in zip(beside(packed, is_west), (p0, cy, cx)):
                dst[rows, at : at + 8] = tile

    @pl.when(first_row)
    def _():
        p1[0:HALO] = jnp.zeros((HALO, WIDE, LANES), F32)

    @pl.when(last_row)
    def _():
        p1[HALO + SIZE :] = jnp.zeros((HALO, WIDE, LANES), F32)

    sub = lax.broadcasted_iota(jnp.int32, (8, LANES), 0)
    lowest, highest = sub == 0, sub == 7
    low_rows, high_rows = jnp.where(first_row, HALO, 0), jnp.where(last_row, HALO + SIZE, TALL)

    def stepped(src, y, tiles):
        j0, j1 = tiles[0], tiles[-1] + 1
        around = range(max(j0 - 1, 0), min(j1 + 1, WIDE // 8))
        at = lambda j: pl.ds(8 * j, 8)
        mid = {j: src[y, at(j)] for j in around}
        up = {j: turned(v, 1) for j, v in mid.items()}
        down = {j: turned(v, -1) for j, v in mid.items()}
        out = []
        for j in tiles:
            below, above = src[y - 1, at(j)], src[y + 1, at(j)]
            left = jnp.where(lowest, up[j - 1], up[j]) if j - 1 in up else up[j]
            right = jnp.where(highest, down[j + 1], down[j]) if j + 1 in down else down[j]
            spread = below + above + left + right - 4.0 * mid[j]
            new = mid[j] - cy[y, at(j)] * (above - below) - cx[y, at(j)] * (right - left) + 0.05 * spread
            if j == 0:
                new = jnp.where(has_west, new, 0.0)
            if j == WIDE // 8 - 1:
                new = jnp.where(has_east, new, 0.0)
            out.append(new)
        return out

    src, dst = p0, p1
    for step in range(1, STEPS):
        tiles = list(range(WIDE // 8))

        def body(y, _, src=src, dst=dst):
            for j, new in zip(tiles, stepped(src, y, tiles)):
                dst[y, pl.ds(8 * j, 8)] = new
            return 0

        lax.fori_loop(jnp.maximum(step, low_rows), jnp.minimum(TALL - step, high_rows), body, 0)
        src, dst = dst, src

    tiles = list(range(1, 1 + SIZE // 8))

    def final(y, _):
        new = stepped(src, y + HALO, tiles)
        moved = [v - GUESS for v in new]
        for j, v in enumerate(new):
            end[y, pl.ds(8 * j, 8)] = v
        total, square = moved[0], moved[0] * moved[0]
        for v in moved[1:]:
            total, square = total + v, square + v * v
        cy[y, 0:8] = total
        cx[y, 0:8] = square
        return 0

    lax.fori_loop(0, SIZE, final, 0)
    total = jnp.sum(cy[0:SIZE, 0:8], axis=1)
    square = jnp.sum(cx[0:SIZE, 0:8], axis=1)
    for k in range(sums.shape[0]):
        sums[k, 0:SIZE] = total
        sums[k, SIZE : 2 * SIZE] = square


def call(kernel, args, outs, scratch, in_specs=None):
    specs = in_specs or [VMEM] * len(args)
    return pl.pallas_call(
        kernel,
        out_shape=[pltpu.VMEM(shape, F32) for shape in outs],
        in_specs=specs,
        out_specs=[VMEM] * len(outs),
        scratch_shapes=scratch,
        compiler_params=pltpu.CompilerParams(vmem_limit_bytes=16 * 2**20),
    )(*[pltpu.with_memory_space_constraint(a, s.memory_space) for a, s in zip(args, specs)])


def shards(tracer, flow_y, flow_x):
    columns, rows = (SIZE, 16, LANES), (16, SIZE, LANES)
    *blocks, col_a, col_b, row_a, row_b = call(
        pack_kernel,
        (tracer, flow_y, flow_x),
        (tracer.shape,) * 3 + (columns,) * 2 + (rows,) * 2,
        [pltpu.SemaphoreType.DMA((3,))],
        in_specs=[pl.BlockSpec(memory_space=pltpu.HBM)] * 3,
    )
    col_a, col_b = swap_with(col_a, COLS, 0), swap_with(col_b, COLS, 1)
    row_a, row_b = swap_with(row_a, ROWS, 0), swap_with(row_b, ROWS, 1)

    cor_a, cor_b = call(corner_kernel, (col_a, col_b), ((STEPS - 1, SIZE, LANES),) * 2, [])
    cor_a, cor_b = swap_with(cor_a, ROWS, 0), swap_with(cor_b, ROWS, 1)
    edges = (col_a, col_b, row_a, row_b, cor_a, cor_b)
    tracer, sums = call(
        steps_kernel,
        (*blocks, *edges),
        (tracer.shape, (lax.axis_size("x"), 2 * SIZE, LANES)),
        [pltpu.VMEM(WORK, F32)] * 4,
    )
    count = SIZE * size_of(COLS)
    sums = lax.all_to_all(sums, "x", 0, 0, tiled=True)
    sums = call(sum_kernel, (sums,), ((lax.axis_size("y"), 2 * SIZE, LANES),), [])[0]
    sums = jnp.sum(lax.all_to_all(sums, "y", 0, 0, tiled=True), axis=0)
    totals, squares = sums[:SIZE, None], sums[SIZE:, None]
    line_mean = GUESS + totals / count
    centred = tracer - line_mean
    line_variance = squares / count - totals / count * (totals / count)
    scaled_field = centred * lax.rsqrt(line_variance + 0.0001)
    return (scaled_field, tracer)


def solution(mesh):
    mesh = Mesh(mesh.devices.reshape(2, 8, 8, 4), ("site", "rows", "y", "x"))
    placed = P(("site", "rows"), COLS, None)
    return jax.shard_map(
        shards, mesh=mesh, in_specs=(placed,) * 3, out_specs=(placed,) * 2, check_vma=False
    )
```

time: 70.9 us -> 62.7 us (0.88)
  blocking collectives: 29.5 us -> 13.1 us
  starting transfers between devices: 12.1 us -> 27.2 us
  Pallas kernels: 0 us -> 7.17 us
  other arithmetic: 6.15 us -> 0.91 us
  waiting for transfers between devices: 17.6 us -> 12.4 us
  local copies, waits for them, and re-layouts: 4.13 us -> 0.79 us
    all_to_all x2 -> x1, blocking collectives: 29.5 us -> 13.1 us  [shards(): sums = lax.all_to_all(sums, 'x', 0, 0, tiled=True)]
    ppermute x4 -> x6, waiting for transfers between devices: 17.6 us -> 2.68 us  [swap_with(): return lax.ppermute(block, axis, pairs)]
    all_to_all x0 -> x1, waiting for transfers between devices: none -> 9.69 us  [shards(): sums = jnp.sum(lax.all_to_all(sums, 'y', 0, 0, tiled=True), axis=0)]
    ppermute x4 -> x6, starting transfers between devices: 12.1 us -> 19.7 us  [swap_with(): return lax.ppermute(block, axis, pairs)]
    all_to_all x0 -> x1, starting transfers between devices: none -> 7.53 us  [shards(): sums = jnp.sum(lax.all_to_all(sums, 'y', 0, 0, tiled=True), axis=0)]
    pallas_call x0 -> x4, Pallas kernels: none -> 7.17 us  [call(): pl.pallas_call(kernel, out_shape=[pltpu.VMEM(shape, F32) for shape in out...]
    select_n x5 -> x0, other arithmetic: 3.47 us -> none  [shards(): values = jnp.where(keep_cells.reshape((-1,) + (1,) * 1), values, 0.0)]
    slice x12 -> x0, local copies, waits for them, and re-layouts: 2.22 us -> none  [the longest x2 2.04 us: shards(): p[size - w:]]
  transfers between devices with their start and end apart: 4 -> 7, of which waited for: 4 -> 2; matrix products, arithmetic and copies ran while one was open for 1% -> 1% of each run, Pallas kernels for 0% -> 0%
where the time goes in v2:
time: 62.7 us; the launch traced here: 62.3 us
  starting transfers between devices  27.2 us (43%)
  blocking collectives  13.1 us (21%)
  waiting for transfers between devices  12.4 us (20%)
  Pallas kernels  7.17 us (11%)
  other arithmetic  0.91 us (1%)
  local copies, waits for them, and re-layouts  0.79 us (1%)
  between operations  0.75 us (1%)
    ppermute x6, starting transfers between devices, swap_with(): return lax.ppermute(block, axis, pairs)  19.7 us
    all_to_all x1, blocking collectives, shards(): sums = lax.all_to_all(sums, 'x', 0, 0, tiled=True)  13.1 us
    all_to_all x1, waiting for transfers between devices, shards(): sums = jnp.sum(lax.all_to_all(sums, 'y', 0, 0, tiled=True), axis=0)  9.69 us
    all_to_all x1, starting transfers between devices, shards(): sums = jnp.sum(lax.all_to_all(sums, 'y', 0, 0, tiled=True), axis=0)  7.53 us
    pallas_call x4, Pallas kernels, call(): pl.pallas_call(kernel, out_shape=[pltpu.VMEM(shape, F32) for shape in out...  7.17 us
    ppermute x6, waiting for transfers between devices, swap_with(): return lax.ppermute(block, axis, pairs)  2.68 us
  transfers between devices with their start and end apart: 7, of which 2 were waited for; matrix products, arithmetic and copies ran while one was open for 1% of the time, Pallas kernels for 0%

profile of v2, /device:TPU:192, one launch (start us, length us, event | category | flops | bytes accessed | tf_op | source)
XLA Modules:
  0.0 62.3 jit_solution(16849347229045387524)
XLA Ops:
  0.6 1.5 %shard_map.50 = (f32[32,32,128]{2,1,0:T(8,128)S(1)}, f32[32,32,128]{2,1,0:T(8,128)S(1)}, f32[32,32,128]{2,1,0:T(8,128)S(1)}, f32[32,16,128]{2,1,0:T(8,128)S(1)},...) custom-call(f32[32,32,128]{2,1,0:T(8,128)} %t_in.1, f32[32,32,128]{2,1,0:T(8,128)} %fy_in.1, ...), custom_call_target="tpu_custom_call" | custom-call | tf_op jit(solution)/shard_map/pallas_call | solution.py:188
  2.1 3.4 %collective-permute-start = (f32[32,16,128]{2,1,0:T(8,128)S(1)}, f32[32,16,128]{2,1,0:T(8,128)S(1)}, u32[]{:S(2)}, u32[]{:S(2)}) collective-permute-start(f32[32,16,128]{2,1,0:T(8,128)S(1)} %get-tuple-element.16), channel_id=1, source_target_pairs={{0,1},{1,0},{2,3},{3,2},{4,5},{5,4},{6,7},{7,6},{8,9},{9,8},{10,11... | collective-permute-start | bytes 786440 | tf_op jit(solution)/shard_map/ppermute | solution.py:35
  5.5 0.7 %collective-permute-start.1 = (f32[32,16,128]{2,1,0:T(8,128)S(1)}, f32[32,16,128]{2,1,0:T(8,128)S(1)}, u32[]{:S(2)}, u32[]{:S(2)}) collective-permute-start(f32[32,16,128]{2,1,0:T(8,128)S(1)} %get-tuple-element.17), channel_id=1, source_target_pairs={{1,2},{2,1},{3,4},{4,3},{5,6},{6,5},{7,8},{8,7},{9,10},{10,9},{11,... | collective-permute-start | bytes 786440 | tf_op jit(solution)/shard_map/ppermute | solution.py:35
  6.2 1.9 %collective-permute-start.2 = (f32[16,32,128]{2,1,0:T(8,128)S(1)}, f32[16,32,128]{2,1,0:T(8,128)S(1)}, u32[]{:S(2)}, u32[]{:S(2)}) collective-permute-start(f32[16,32,128]{2,1,0:T(8,128)S(1)} %get-tuple-element.18), channel_id=1, source_target_pairs={{0,32},{32,0},{64,96},{96,64},{128,160},{160,128},{192,224},{224,1... | collective-permute-start | bytes 786440 | tf_op jit(solution)/shard_map/ppermute | solution.py:35
  8.1 7.0 %collective-permute-start.3 = (f32[16,32,128]{2,1,0:T(8,128)S(1)}, f32[16,32,128]{2,1,0:T(8,128)S(1)}, u32[]{:S(2)}, u32[]{:S(2)}) collective-permute-start(f32[16,32,128]{2,1,0:T(8,128)S(1)} %get-tuple-element.19), channel_id=1, source_target_pairs={{32,64},{64,32},{96,128},{128,96},{160,192},{192,160},{33,65},{65,... | collective-permute-start | bytes 786440 | tf_op jit(solution)/shard_map/ppermute | solution.py:35
  15.1 0.0 collective-permute-done.col_a
  15.1 0.0 collective-permute-done.1.col_b
  15.2 1.9 %collective-permute-start.4 = (f32[5,32,128]{2,1,0:T(8,128)S(1)}, f32[5,32,128]{2,1,0:T(8,128)S(1)}, u32[]{:S(2)}, u32[]{:S(2)}) collective-permute-start(f32[5,32,128]{2,1,0:T(8,128)S(1)} %get-tuple-element.20), channel_id=1, source_target_pairs={{0,32},{32,0},{64,96},{96,64},{128,160},{160,128},{192,224},{224,1... | collective-permute-start | bytes 245768 | tf_op jit(solution)/shard_map/ppermute | solution.py:35
  17.1 4.8 %collective-permute-start.5 = (f32[5,32,128]{2,1,0:T(8,128)S(1)}, f32[5,32,128]{2,1,0:T(8,128)S(1)}, u32[]{:S(2)}, u32[]{:S(2)}) collective-permute-start(f32[5,32,128]{2,1,0:T(8,128)S(1)} %get-tuple-element.21), channel_id=1, source_target_pairs={{32,64},{64,32},{96,128},{128,96},{160,192},{192,160},{33,65},{65,... | collective-permute-start | bytes 245768 | tf_op jit(solution)/shard_map/ppermute | solution.py:35
  21.9 0.0 collective-permute-done.2.row_a
  22.0 0.0 collective-permute-done.3.row_b
  22.0 0.0 collective-permute-done.4.cor_a
  22.0 2.7 %collective-permute-done.5.cor_b = f32[5,32,128]{2,1,0:T(8,128)S(1)} collective-permute-done((f32[5,32,128]{2,1,0:T(8,128)S(1)}, f32[5,32,128]{2,1,0:T(8,128)S(1)}, u32[]{:S(2)}, u32[]{:S(2)}) %collective-permute-start.5) | collective-permute-done | bytes 81952 | tf_op jit(solution)/shard_map/ppermute | solution.py:35
  24.6 4.9 %shard_map.52 = (f32[32,32,128]{2,1,0:T(8,128)S(1)}, f32[4,64,128]{2,1,0:T(8,128)S(1)}) custom-call(f32[32,32,128]{2,1,0:T(8,128)S(1)} %get-tuple-element.13.t, f32[32,32,128]{2,1,0:T(8,128)S(1)} %get-tuple-element.14.fy, f32[32,32,128]{2,1,0:T(8,128)S(1)} %get-tuple-element.15.fx, f32[32,16,128]{2,1,0:T(8,128)S(1)} %collective-permute-done.col_a, ...), custom_call_target="tpu_custom_call" | custom-call | tf_op jit(solution)/shard_map/pallas_call | solution.py:188
  29.6 13.1 %all_to_all.10.parts = f32[4,64,128]{2,1,0:T(8,128)S(1)} all-to-all(f32[4,64,128]{2,1,0:T(8,128)S(1)} %get-tuple-element.23), channel_id=1, replica_groups=mesh['site'=2,'rows'=8,'y'=8,'x'=4] {'x'}, dimensions={0} | all-to-all | bytes 262144 | tf_op jit(solution)/shard_map/all_to_all | solution.py:220
  42.7 0.7 %shard_map.53 = f32[8,64,128]{2,1,0:T(8,128)} custom-call(f32[4,64,128]{2,1,0:T(8,128)S(1)} %all_to_all.10.parts), custom_call_target="tpu_custom_call" | custom-call | tf_op jit(solution)/shard_map/pallas_call | solution.py:188
  43.4 7.5 %all-to-all-start.1 = ((f32[8,64,128]{2,1,0:T(8,128)}), f32[8,64,128]{2,1,0:T(8,128)S(1)}, u32[]{:S(2)}, u32[]{:S(2)}) async-start(f32[8,64,128]{2,1,0:T(8,128)} %shard_map.53), calls=%async_computation.1 | async-start | bytes 524288 | tf_op jit(solution)/shard_map/all_to_all | solution.py:222
  50.9 0.8 %copy.5 = f32[32,32,128]{2,1,0:T(8,128)} copy(f32[32,32,128]{2,1,0:T(8,128)S(1)} %get-tuple-element.27) | data formatting | bytes 1048576
  51.7 9.7 %all-to-all-done.1 = f32[8,64,128]{2,1,0:T(8,128)S(1)} async-done(((f32[8,64,128]{2,1,0:T(8,128)}), f32[8,64,128]{2,1,0:T(8,128)S(1)}, u32[]{:S(2)}, u32[]{:S(2)}) %all-to-all-start.1) | async-done | bytes 262176 | tf_op jit(solution)/shard_map/all_to_all | solution.py:222
  61.5 0.9 %subtract_multiply_fusion = f32[32,32,128]{2,1,0:T(8,128)} fusion(f32[32,32,128]{2,1,0:T(8,128)S(1)} %get-tuple-element.27, f32[32,128]{1,0:T(8,128)S(1)} %get-tuple-element.25, f32[32,128]{1,0:T(8,128)S(1)} %get-tuple-element.24), kind=kLoop, calls=%fused_computation | loop fusion | flops 262144 | bytes 1081344 | tf_op jit(solution)/shard_map/mul | solution.py:227
  (3 shorter events, 0.1 us)
Async XLA Ops:
  2.1 13.0 %collective-permute-start = (f32[32,16,128]{2,1,0:T(8,128)S(1)}, f32[32,16,128]{2,1,0:T(8,128)S(1)}, u32[]{:S(2)}, u32[]{:S(2)}) collective-permute-start(f32[32,16,128]{2,1,0:T(8,128)S(1)} %get-tuple-element.16), channel_id=1, source_target_pairs={{0,1},{1,0},{2,3},{3,2},{4,5},{5,4},{6,7},{7,6},{8,9},{9,8},{10,11... | collective-permute-start | bytes 786440 | tf_op jit(solution)/shard_map/ppermute | solution.py:35
  5.5 9.6 %collective-permute-start.1 = (f32[32,16,128]{2,1,0:T(8,128)S(1)}, f32[32,16,128]{2,1,0:T(8,128)S(1)}, u32[]{:S(2)}, u32[]{:S(2)}) collective-permute-start(f32[32,16,128]{2,1,0:T(8,128)S(1)} %get-tuple-element.17), channel_id=1, source_target_pairs={{1,2},{2,1},{3,4},{4,3},{5,6},{6,5},{7,8},{8,7},{9,10},{10,9},{11,... | collective-permute-start | bytes 786440 | tf_op jit(solution)/shard_map/ppermute | solution.py:35
  6.2 15.7 %collective-permute-start.2 = (f32[16,32,128]{2,1,0:T(8,128)S(1)}, f32[16,32,128]{2,1,0:T(8,128)S(1)}, u32[]{:S(2)}, u32[]{:S(2)}) collective-permute-start(f32[16,32,128]{2,1,0:T(8,128)S(1)} %get-tuple-element.18), channel_id=1, source_target_pairs={{0,32},{32,0},{64,96},{96,64},{128,160},{160,128},{192,224},{224,1... | collective-permute-start | bytes 786440 | tf_op jit(solution)/shard_map/ppermute | solution.py:35
  8.1 13.8 %collective-permute-start.3 = (f32[16,32,128]{2,1,0:T(8,128)S(1)}, f32[16,32,128]{2,1,0:T(8,128)S(1)}, u32[]{:S(2)}, u32[]{:S(2)}) collective-permute-start(f32[16,32,128]{2,1,0:T(8,128)S(1)} %get-tuple-element.19), channel_id=1, source_target_pairs={{32,64},{64,32},{96,128},{128,96},{160,192},{192,160},{33,65},{65,... | collective-permute-start | bytes 786440 | tf_op jit(solution)/shard_map/ppermute | solution.py:35
  15.2 6.8 %collective-permute-start.4 = (f32[5,32,128]{2,1,0:T(8,128)S(1)}, f32[5,32,128]{2,1,0:T(8,128)S(1)}, u32[]{:S(2)}, u32[]{:S(2)}) collective-permute-start(f32[5,32,128]{2,1,0:T(8,128)S(1)} %get-tuple-element.20), channel_id=1, source_target_pairs={{0,32},{32,0},{64,96},{96,64},{128,160},{160,128},{192,224},{224,1... | collective-permute-start | bytes 245768 | tf_op jit(solution)/shard_map/ppermute | solution.py:35
  17.1 7.5 %collective-permute-start.5 = (f32[5,32,128]{2,1,0:T(8,128)S(1)}, f32[5,32,128]{2,1,0:T(8,128)S(1)}, u32[]{:S(2)}, u32[]{:S(2)}) collective-permute-start(f32[5,32,128]{2,1,0:T(8,128)S(1)} %get-tuple-element.21), channel_id=1, source_target_pairs={{32,64},{64,32},{96,128},{128,96},{160,192},{192,160},{33,65},{65,... | collective-permute-start | bytes 245768 | tf_op jit(solution)/shard_map/ppermute | solution.py:35
  43.4 18.0 %all-to-all-start.1 = ((f32[8,64,128]{2,1,0:T(8,128)}), f32[8,64,128]{2,1,0:T(8,128)S(1)}, u32[]{:S(2)}, u32[]{:S(2)}) async-start(f32[8,64,128]{2,1,0:T(8,128)} %shard_map.53), calls=%async_computation.1 | async-start | bytes 524288 | tf_op jit(solution)/shard_map/all_to_all | solution.py:222

commit v3 on v2

v3 whole, which is shorter than its diff:
```python
import functools

import jax
import jax.numpy as jnp
from jax import lax
from jax.experimental import pallas as pl
from jax.experimental.pallas import tpu as pltpu
from jax.sharding import Mesh, PartitionSpec as P

STEPS = 6
SIZE = 32
LANES = 128
ROWS = "rows"
COLS = ("y", "x")
HALO = STEPS
TALL = SIZE + 2 * HALO
WIDE = SIZE + 16
BLOCK = slice(HALO, HALO + SIZE)
CENTRE = slice(8, 8 + SIZE)
WORK = (TALL, WIDE, LANES)
GUESS = 1.0
OUTER = WIDE // 8 - 1
F32 = jnp.float32
VMEM = pl.BlockSpec(memory_space=pltpu.VMEM)


def size_of(axis):
    sizes = [lax.axis_size(a) for a in ((axis,) if isinstance(axis, str) else axis)]
    return functools.reduce(lambda a, b: a * b, sizes)


def swap_with(block, axis, odd):
    pairs = []
    for low in range(odd, size_of(axis) - 1, 2):
        pairs += [(low, low + 1), (low + 1, low)]
    return lax.ppermute(block, axis, pairs)


def turned(tiles, shift):
    return pltpu.roll(tiles, shift % 8, axis=tiles.ndim - 2)


def pack_kernel(t_in, fy_in, fx_in, t, fy, fx, col_a, col_b, row_a, row_b, sems):
    blocks = ((t_in, t), (fy_in, fy), (fx_in, fx))
    copies = [pltpu.make_async_copy(src, dst, sems.at[k]) for k, (src, dst) in enumerate(blocks)]
    for copy in copies:
        copy.start()
    even_row = lax.axis_index(ROWS) % 2 == 0
    even_col = lax.axis_index(COLS) % 2 == 0
    sub = lax.broadcasted_iota(jnp.int32, (SIZE, 8, LANES), 1)
    for copy in copies:
        copy.wait()
    t_low, fy_low, fx_low = [v[:, 0:8] for v in (t, fy, fx)]
    t_high, fy_high, fx_high = [v[:, SIZE - 8 :] for v in (t, fy, fx)]
    first = (
        jnp.where(sub < 6, t_low, turned(fx_low, 6)),
        jnp.where(sub < 5, fy_low, turned(fx_low, 3)),
    )
    last = (
        jnp.where(sub >= 2, t_high, turned(fx_high, 5)),
        jnp.where(sub >= 3, fy_high, turned(fx_high, 3)),
    )
    for k in range(2):
        col_a[:, 8 * k : 8 * k + 8] = jnp.where(even_col, last[k], first[k])
        col_b[:, 8 * k : 8 * k + 8] = jnp.where(even_col, first[k], last[k])
    for out, top in ((row_a, even_row), (row_b, jnp.logical_not(even_row))):
        out[0:6] = t[pl.ds(jnp.where(top, SIZE - 6, 0), 6)]
        out[6:11] = fy[pl.ds(jnp.where(top, SIZE - 5, 0), 5)]
        out[11:16] = fx[pl.ds(jnp.where(top, SIZE - 5, 0), 5)]


def corner_kernel(col_a, col_b, cor_a, cor_b):
    even_row = lax.axis_index(ROWS) % 2 == 0
    for out, top in ((cor_a, even_row), (cor_b, jnp.logical_not(even_row))):
        at = pl.ds(jnp.where(top, SIZE - STEPS + 1, 0), STEPS - 1)
        out[:, 0:16] = col_a[at]
        out[:, 16:32] = col_b[at]


def sum_kernel(parts, out):
    total = jnp.sum(parts[...], axis=0)
    for k in range(out.shape[0]):
        out[k] = total


def scale_kernel(tracer, parts, scaled_out, end_out, scaled, mean, rate, sems):
    whole = pltpu.make_async_copy(tracer, end_out, sems.at[0])
    whole.start()
    sums = jnp.sum(parts[...], axis=0)
    count = SIZE * size_of(COLS)
    off = sums[:SIZE] / count
    mean[...] = GUESS + off
    rate[...] = lax.rsqrt(sums[SIZE:] / count - off * off + 0.0001)
    copies = [whole]
    for k in range(4):
        some = pl.ds(k * (SIZE // 4), SIZE // 4)
        for y in range(k * (SIZE // 4), (k + 1) * (SIZE // 4)):
            scaled[y] = (tracer[y] - mean[pl.ds(y, 1)]) * rate[pl.ds(y, 1)]
        copies.append(pltpu.make_async_copy(scaled.at[some], scaled_out.at[some], sems.at[1 + k]))
        copies[-1].start()
    for copy in copies:
        copy.wait()


def beside(packed, west):
    one, two = packed[:, 0:8], packed[:, 8:16]
    sub = lax.broadcasted_iota(jnp.int32, one.shape, 1)
    if west:
        return one, two, jnp.where(sub < 5, turned(one, 3), turned(two, 5))
    return one, two, jnp.where(sub < 2, turned(one, 2), turned(two, 5))


def moved_on(mid, below, above, left, right, flow_y, flow_x):
    spread = (below + above) + (left + right)
    return 0.8 * mid + 0.05 * spread - flow_y * (above - below) - flow_x * (right - left)


def sides():
    row, col = lax.axis_index(ROWS), lax.axis_index(COLS)
    return row == 0, row == lax.axis_size(ROWS) - 1, col > 0, col < size_of(COLS) - 1


def at(j):
    return pl.ds(8 * j, 8)


def sublanes():
    sub = lax.broadcasted_iota(jnp.int32, (8, LANES), 0)
    return sub == 0, sub == 7


def steps_kernel(t, fy, fx, col_a, col_b, row_a, row_b, p0, p1, p2, p3, p4, p5, cy, cx, end, sums, total, square):
    even_row, even_col = lax.axis_index(ROWS) % 2 == 0, lax.axis_index(COLS) % 2 == 0
    first_row, last_row, has_west, has_east = sides()
    for src, dst in ((t, p0), (fy, cy), (fx, cx)):
        dst[BLOCK, CENTRE] = src[...]
    west, east = jnp.where(even_col, col_b[...], col_a[...]), jnp.where(even_col, col_a[...], col_b[...])
    for v, j, is_west in ((west, 0, True), (east, OUTER, False)):
        for tile, dst in zip(beside(v, is_west), (p0, cy, cx)):
            dst[BLOCK, at(j)] = tile
    south, north = jnp.where(even_row, row_b[...], row_a[...]), jnp.where(even_row, row_a[...], row_b[...])
    for (b, e), dst in zip(((0, 6), (6, 11), (11, 16)), (p0, cy, cx)):
        dst[HALO - (e - b) : HALO, CENTRE] = south[b:e]
        dst[HALO + SIZE : HALO + SIZE + e - b, CENTRE] = north[b:e]
    lowest, highest = sublanes()

    def stepped(src, y, tiles):
        around = [j for j in range(tiles[0] - 1, tiles[-1] + 2) if 0 <= j <= OUTER]
        mid = {j: src[y, at(j)] for j in around}
        up = {j: turned(v, 1) for j, v in mid.items()}
        down = {j: turned(v, -1) for j, v in mid.items()}
        out = []
        for j in tiles:
            left = jnp.where(lowest, up[j - 1], up[j]) if j > 0 else up[j]
            right = jnp.where(highest, down[j + 1], down[j]) if j < OUTER else down[j]
            new = moved_on(mid[j], src[y - 1, at(j)], src[y + 1, at(j)], left, right, cy[y, at(j)], cx[y, at(j)])
            if j == 0:
                new = jnp.where(has_west, new, 0.0)
            if j == OUTER:
                new = jnp.where(has_east, new, 0.0)
            out.append(new)
        return out

    fields = (p0, p1, p2, p3, p4, p5)
    middle, everything = list(range(1, OUTER)), list(range(OUTER + 1))
    for step, (src, dst) in enumerate(zip(fields, fields[1:]), start=1):
        for y in list(range(step, HALO)) + list(range(HALO + SIZE, TALL - step)):
            outside = first_row if y < HALO else last_row
            for j, new in zip(middle, stepped(src, y, middle)):
                dst[y, at(j)] = jnp.where(outside, 0.0, new)

        def body(i, _, src=src, dst=dst):
            for y in (2 * i + HALO, 2 * i + HALO + 1):
                for j, new in zip(everything, stepped(src, y, everything)):
                    dst[y, at(j)] = new
            return 0

        lax.fori_loop(0, SIZE // 2, body, 0)

    def final(i, _):
        for y in (2 * i, 2 * i + 1):
            new = stepped(p5, y + HALO, middle)
            for j, v in zip(middle, new):
                end[y, at(j - 1)] = v
            total[y], square[y] = moments(new)
        return 0

    lax.fori_loop(0, SIZE // 2, final, 0)
    sums[0:SIZE] = jnp.sum(total[...], axis=1)
    sums[SIZE : 2 * SIZE] = jnp.sum(square[...], axis=1)


def moments(tiles):
    moved = [v - GUESS for v in tiles]
    squares = [v * v for v in moved]
    add = lambda v: functools.reduce(lambda a, b: a + b, v)
    return add(moved), add(squares)


def patch_kernel(p0, p1, p2, p3, p4, p5, cy, cx, cor_a, cor_b, end, sums, end_out, sums_out, total, square):
    even_row, even_col = lax.axis_index(ROWS) % 2 == 0, lax.axis_index(COLS) % 2 == 0
    first_row, last_row, has_west, has_east = sides()
    lowest, highest = sublanes()
    fields = (p0, p1, p2, p3, p4, p5)
    end_out[...] = end[...]
    for k in range(sums_out.shape[0]):
        sums_out[k] = sums[...]
    south, north = jnp.where(even_row, cor_b[...], cor_a[...]), jnp.where(even_row, cor_a[...], cor_b[...])
    for is_south, corner, outside in ((True, south, first_row), (False, north, last_row)):
        row = (lambda r: r) if is_south else (lambda r: TALL - 1 - r)
        inner_tiles = {}
        for is_west, inside in ((True, has_west), (False, has_east)):
            packed = jnp.where(even_col == is_west, corner[:, 16:32], corner[:, 0:16])
            order = list(range(HALO - 1)) if is_south else list(range(HALO - 1))[::-1]
            tracer, flow_y, flow_x = [
                {r: tile[i] for r, i in enumerate(order, start=1)} for tile in beside(packed, is_west)
            ]
            j0, j1, j2 = (0, 1, 2) if is_west else (OUTER, OUTER - 1, OUTER - 2)
            tracer[0] = jnp.zeros((8, LANES), F32)
            fixed = {(r, j0): v for r, v in tracer.items()}
            for step in range(1, STEPS + 1):
                field = fields[step - 1]
                get = lambda r, j: fixed[r, j] if (r, j) in fixed else field[row(r), at(j)]
                now = {}
                for r in range(step, HALO + step):
                    for j in (j0, j1) if step < STEPS else (j1,):
                        mid = get(r, j)
                        near, far = (get(r, j2 if j == j1 else j1), get(r, j0) if j == j1 else mid)
                        lower, higher = (far, near) if is_west else (near, far)
                        left = jnp.where(lowest, turned(lower, 1), turned(mid, 1)) if lower is not mid else turned(mid, 1)
                        right = jnp.where(highest, turned(higher, -1), turned(mid, -1)) if higher is not mid else turned(mid, -1)
                        below, above = (get(r - 1, j), get(r + 1, j)) if is_south else (get(r + 1, j), get(r - 1, j))
                        of_corner = j == j0 and r < HALO
                        flows = (flow_y[r], flow_x[r]) if of_corner else (cy[row(r), at(j)], cx[row(r), at(j)])
                        new = moved_on(mid, below, above, left, right, *flows)
                        if j == j0:
                            new = jnp.where(inside, new, 0.0)
                        if r < HALO:
                            new = jnp.where(outside, 0.0, new)
                        now[r, j] = new
                fixed = now
            for r in range(HALO, 2 * HALO):
                inner_tiles[r, j1] = fixed[r, j1]
        for r in range(HALO, 2 * HALO):
            y = row(r) - HALO
            new = [inner_tiles[r, j] if (r, j) in inner_tiles else end[y, at(j - 1)] for j in range(1, OUTER)]
            for j in (1, OUTER - 1):
                end_out[y, at(j - 1)] = new[j - 1]
            i = y if is_south else y - SIZE + 2 * HALO
            total[i], square[i] = moments(new)
    total, square = jnp.sum(total[...], axis=1), jnp.sum(square[...], axis=1)
    for k in range(sums_out.shape[0]):
        for b, v in ((0, total), (SIZE, square)):
            sums_out[k, b : b + HALO] = v[:HALO]
            sums_out[k, b + SIZE - HALO : b + SIZE] = v[HALO:]


def call(kernel, args, outs, scratch, in_specs=None):
    specs = in_specs or [VMEM] * len(args)
    return pl.pallas_call(
        kernel,
        out_shape=[pltpu.VMEM(shape, F32) for shape in outs],
        in_specs=specs,
        out_specs=[VMEM] * len(outs),
        scratch_shapes=scratch,
        compiler_params=pltpu.CompilerParams(vmem_limit_bytes=16 * 2**20),
    )(*[pltpu.with_memory_space_constraint(a, s.memory_space) for a, s in zip(args, specs)])


def shards(tracer, flow_y, flow_x):
    columns, rows = (SIZE, 16, LANES), (16, SIZE, LANES)
    *blocks, col_a, col_b, row_a, row_b = call(
        pack_kernel,
        (tracer, flow_y, flow_x),
        (tracer.shape,) * 3 + (columns,) * 2 + (rows,) * 2,
        [pltpu.SemaphoreType.DMA((3,))],
        in_specs=[pl.BlockSpec(memory_space=pltpu.HBM)] * 3,
    )
    col_a, col_b = swap_with(col_a, COLS, 0), swap_with(col_b, COLS, 1)
    row_a, row_b = swap_with(row_a, ROWS, 0), swap_with(row_b, ROWS, 1)

    cor_a, cor_b = call(corner_kernel, (col_a, col_b), ((STEPS - 1, SIZE, LANES),) * 2, [])
    cor_a, cor_b = swap_with(cor_a, ROWS, 0), swap_with(cor_b, ROWS, 1)
    partial = pltpu.VMEM((SIZE, 8, LANES), F32)
    *fields, tracer, sums = call(
        steps_kernel,
        (*blocks, col_a, col_b, row_a, row_b),
        (WORK,) * (STEPS + 2) + (tracer.shape, (2 * SIZE, LANES)),
        [partial] * 2,
    )
    partial = pltpu.VMEM((2 * HALO, 8, LANES), F32)
    tracer, sums = call(
        patch_kernel,
        (*fields, cor_a, cor_b, tracer, sums),
        (tracer.shape, (lax.axis_size("x"), 2 * SIZE, LANES)),
        [partial] * 2,
    )
    sums = lax.all_to_all(sums, "x", 0, 0, tiled=True)
    sums = call(sum_kernel, (sums,), ((lax.axis_size("y"), 2 * SIZE, LANES),), [])[0]
    sums = lax.all_to_all(sums, "y", 0, 0, tiled=True)
    outer = pl.BlockSpec(memory_space=pltpu.HBM)
    return tuple(
        pl.pallas_call(
            scale_kernel,
            out_shape=[jax.ShapeDtypeStruct(tracer.shape, F32)] * 2,
            in_specs=[VMEM] * 2,
            out_specs=[outer] * 2,
            scratch_shapes=[
                pltpu.VMEM(tracer.shape, F32),
                pltpu.VMEM((SIZE, LANES), F32),
                pltpu.VMEM((SIZE, LANES), F32),
                pltpu.SemaphoreType.DMA((5,)),
            ],
            compiler_params=pltpu.CompilerParams(vmem_limit_bytes=16 * 2**20),
        )(*[pltpu.with_memory_space_constraint(v, pltpu.VMEM) for v in (tracer, sums)])
    )


def solution(mesh):
    mesh = Mesh(mesh.devices.reshape(2, 8, 8, 4), ("site", "rows", "y", "x"))
    placed = P(("site", "rows"), COLS, None)
    return jax.shard_map(
        shards, mesh=mesh, in_specs=(placed,) * 3, out_specs=(placed,) * 2, check_vma=False
    )
```

time: 62.7 us -> 59 us (0.941)
  blocking collectives: 13.1 us -> 31.2 us
  waiting for transfers between devices: 12.4 us -> 0.02 us
  starting transfers between devices: 27.2 us -> 19.7 us
  other arithmetic: 0.91 us -> 0 us
  local copies, waits for them, and re-layouts: 0.79 us -> 0 us
    all_to_all x0 -> x1, blocking collectives: none -> 17.8 us  [shards(): sums = lax.all_to_all(sums, 'y', 0, 0, tiled=True)]
    all_to_all x1 -> x0, waiting for transfers between devices: 9.69 us -> none  [shards(): sums = jnp.sum(lax.all_to_all(sums, 'y', 0, 0, tiled=True), axis=0)]
    all_to_all x1 -> x0, starting transfers between devices: 7.53 us -> none  [shards(): sums = jnp.sum(lax.all_to_all(sums, 'y', 0, 0, tiled=True), axis=0)]
    ppermute x6, waiting for transfers between devices: 2.68 us -> 0.02 us  [swap_with(): return lax.ppermute(block, axis, pairs)]
    pallas_call x4 -> x5, Pallas kernels: 7.17 us -> 5.94 us  [call(): pl.pallas_call(kernel, out_shape=[pltpu.VMEM(shape, F32) for shape in out...]
    pallas_call x0 -> x1, Pallas kernels: none -> 1 us  [shards(): pl.pallas_call(scale_kernel, out_shape=[jax.ShapeDtypeStruct(tracer.shape...]
    mul x1 -> x0, other arithmetic: 0.88 us -> none  [shards(): scaled_field = centred * lax.rsqrt(line_variance + 0.0001)]
    unnamed x1 -> x0, local copies, waits for them, and re-layouts: 0.79 us -> none
  transfers between devices with their start and end apart: 7 -> 6, of which waited for: 2 -> 0; matrix products, arithmetic and copies ran while one was open for 1% -> 0% of each run, Pallas kernels for 0% -> 6%
where the time goes in v3:
time: 59 us; the launch traced here: 58.6 us
  blocking collectives  31.2 us (53%)
  starting transfers between devices  19.7 us (33%)
  Pallas kernels  6.93 us (12%)
  between operations  0.76 us (1%)
    ppermute x6, starting transfers between devices, swap_with(): return lax.ppermute(block, axis, pairs)  19.7 us
    all_to_all x1, blocking collectives, shards(): sums = lax.all_to_all(sums, 'y', 0, 0, tiled=True)  17.8 us
    all_to_all x1, blocking collectives, shards(): sums = lax.all_to_all(sums, 'x', 0, 0, tiled=True)  13.4 us
    pallas_call x5, Pallas kernels, call(): pl.pallas_call(kernel, out_shape=[pltpu.VMEM(shape, F32) for shape in out...  5.94 us
  transfers between devices with their start and end apart: 6, of which 0 were waited for; matrix products, arithmetic and copies ran while one was open for 0% of the time, Pallas kernels for 6%

profile of v3, /device:TPU:192, one launch (start us, length us, event | category | flops | bytes accessed | tf_op | source)
XLA Modules:
  0.0 58.6 jit_solution(2540847797780107585)
XLA Ops:
  0.6 1.5 %shard_map.50 = (f32[32,32,128]{2,1,0:T(8,128)S(1)}, f32[32,32,128]{2,1,0:T(8,128)S(1)}, f32[32,32,128]{2,1,0:T(8,128)S(1)}, f32[32,16,128]{2,1,0:T(8,128)S(1)},...) custom-call(f32[32,32,128]{2,1,0:T(8,128)} %t_in.1, f32[32,32,128]{2,1,0:T(8,128)} %fy_in.1, ...), custom_call_target="tpu_custom_call" | custom-call | tf_op jit(solution)/shard_map/pallas_call | solution.py:260
  2.1 3.4 %collective-permute-start = (f32[32,16,128]{2,1,0:T(8,128)S(1)}, f32[32,16,128]{2,1,0:T(8,128)S(1)}, u32[]{:S(2)}, u32[]{:S(2)}) collective-permute-start(f32[32,16,128]{2,1,0:T(8,128)S(1)} %get-tuple-element.26), channel_id=1, source_target_pairs={{0,1},{1,0},{2,3},{3,2},{4,5},{5,4},{6,7},{7,6},{8,9},{9,8},{10,11... | collective-permute-start | bytes 786440 | tf_op jit(solution)/shard_map/ppermute | solution.py:36
  5.5 0.7 %collective-permute-start.1 = (f32[32,16,128]{2,1,0:T(8,128)S(1)}, f32[32,16,128]{2,1,0:T(8,128)S(1)}, u32[]{:S(2)}, u32[]{:S(2)}) collective-permute-start(f32[32,16,128]{2,1,0:T(8,128)S(1)} %get-tuple-element.27), channel_id=1, source_target_pairs={{1,2},{2,1},{3,4},{4,3},{5,6},{6,5},{7,8},{8,7},{9,10},{10,9},{11,... | collective-permute-start | bytes 786440 | tf_op jit(solution)/shard_map/ppermute | solution.py:36
  6.2 1.9 %collective-permute-start.2 = (f32[16,32,128]{2,1,0:T(8,128)S(1)}, f32[16,32,128]{2,1,0:T(8,128)S(1)}, u32[]{:S(2)}, u32[]{:S(2)}) collective-permute-start(f32[16,32,128]{2,1,0:T(8,128)S(1)} %get-tuple-element.28), channel_id=1, source_target_pairs={{0,32},{32,0},{64,96},{96,64},{128,160},{160,128},{192,224},{224,1... | collective-permute-start | bytes 786440 | tf_op jit(solution)/shard_map/ppermute | solution.py:36
  8.1 7.0 %collective-permute-start.3 = (f32[16,32,128]{2,1,0:T(8,128)S(1)}, f32[16,32,128]{2,1,0:T(8,128)S(1)}, u32[]{:S(2)}, u32[]{:S(2)}) collective-permute-start(f32[16,32,128]{2,1,0:T(8,128)S(1)} %get-tuple-element.29), channel_id=1, source_target_pairs={{32,64},{64,32},{96,128},{128,96},{160,192},{192,160},{33,65},{65,... | collective-permute-start | bytes 786440 | tf_op jit(solution)/shard_map/ppermute | solution.py:36
  15.1 0.0 collective-permute-done.col_a
  15.1 0.0 collective-permute-done.1.col_b
  15.2 1.9 %collective-permute-start.4 = (f32[5,32,128]{2,1,0:T(8,128)S(1)}, f32[5,32,128]{2,1,0:T(8,128)S(1)}, u32[]{:S(2)}, u32[]{:S(2)}) collective-permute-start(f32[5,32,128]{2,1,0:T(8,128)S(1)} %get-tuple-element.38), channel_id=1, source_target_pairs={{0,32},{32,0},{64,96},{96,64},{128,160},{160,128},{192,224},{224,1... | collective-permute-start | bytes 245768 | tf_op jit(solution)/shard_map/ppermute | solution.py:36
  17.1 4.8 %collective-permute-start.5 = (f32[5,32,128]{2,1,0:T(8,128)S(1)}, f32[5,32,128]{2,1,0:T(8,128)S(1)}, u32[]{:S(2)}, u32[]{:S(2)}) collective-permute-start(f32[5,32,128]{2,1,0:T(8,128)S(1)} %get-tuple-element.39), channel_id=1, source_target_pairs={{32,64},{64,32},{96,128},{128,96},{160,192},{192,160},{33,65},{65,... | collective-permute-start | bytes 245768 | tf_op jit(solution)/shard_map/ppermute | solution.py:36
  21.9 0.0 collective-permute-done.2.row_a
  22.0 0.0 collective-permute-done.3.row_b
  22.0 3.7 %shard_map.51 = (f32[44,48,128]{2,1,0:T(8,128)S(1)}, f32[44,48,128]{2,1,0:T(8,128)S(1)}, f32[44,48,128]{2,1,0:T(8,128)S(1)}, f32[44,48,128]{2,1,0:T(8,128)S(1)},...) custom-call(f32[32,32,128]{2,1,0:T(8,128)S(1)} %get-tuple-element.23, ...), custom_call_target="tpu_custom_call" | custom-call | tf_op jit(solution)/shard_map/pallas_call | solution.py:260
  25.7 0.0 collective-permute-done.4.cor_a
  25.7 0.0 collective-permute-done.5.cor_b
  25.7 0.7 %shard_map.53 = (f32[32,32,128]{2,1,0:T(8,128)S(1)}, f32[4,64,128]{2,1,0:T(8,128)S(1)}) custom-call(f32[44,48,128]{2,1,0:T(8,128)S(1)} %get-tuple-element.30.p0, f32[44,48,128]{2,1,0:T(8,128)S(1)} %get-tuple-element.31.p1, f32[44,48,128]{2,1,0:T(8,128)S(1)} %get-tuple-element.32.p2, f32[44,48,128]{2,1,0:T(8,128)S(1)} %get-tuple-element.33.p3, ...), custom_call_target="tpu_custom_call" | custom-call | tf_op jit(solution)/shard_map/pallas_call | solution.py:260
  26.4 13.4 %all_to_all.10.parts = f32[4,64,128]{2,1,0:T(8,128)S(1)} all-to-all(f32[4,64,128]{2,1,0:T(8,128)S(1)} %get-tuple-element.43), channel_id=1, replica_groups=mesh['site'=2,'rows'=8,'y'=8,'x'=4] {'x'}, dimensions={0} | all-to-all | bytes 262144 | tf_op jit(solution)/shard_map/all_to_all | solution.py:298
  39.8 17.8 %all_to_all.11.parts = f32[8,64,128]{2,1,0:T(8,128)S(1)} all-to-all(f32[8,64,128]{2,1,0:T(8,128)S(1)} %shard_map.54), channel_id=1, replica_groups=mesh['site'=2,'rows'=8,'y'=8,'x'=4] {'y'}, dimensions={0} | all-to-all | bytes 524288 | tf_op jit(solution)/shard_map/all_to_all | solution.py:300
  57.6 1.0 %shard_map.55 = (f32[32,32,128]{2,1,0:T(8,128)}, f32[32,32,128]{2,1,0:T(8,128)}) custom-call(f32[32,32,128]{2,1,0:T(8,128)S(1)} %get-tuple-element.42.tracer, f32[8,64,128]{2,1,0:T(8,128)S(1)} %all_to_all.11.parts), custom_call_target="tpu_custom_call" | custom-call | tf_op jit(solution)/shard_map/pallas_call | solution.py:303
  (2 shorter events, 0.1 us)
Async XLA Ops:
  2.1 13.0 %collective-permute-start = (f32[32,16,128]{2,1,0:T(8,128)S(1)}, f32[32,16,128]{2,1,0:T(8,128)S(1)}, u32[]{:S(2)}, u32[]{:S(2)}) collective-permute-start(f32[32,16,128]{2,1,0:T(8,128)S(1)} %get-tuple-element.26), channel_id=1, source_target_pairs={{0,1},{1,0},{2,3},{3,2},{4,5},{5,4},{6,7},{7,6},{8,9},{9,8},{10,11... | collective-permute-start | bytes 786440 | tf_op jit(solution)/shard_map/ppermute | solution.py:36
  5.5 9.6 %collective-permute-start.1 = (f32[32,16,128]{2,1,0:T(8,128)S(1)}, f32[32,16,128]{2,1,0:T(8,128)S(1)}, u32[]{:S(2)}, u32[]{:S(2)}) collective-permute-start(f32[32,16,128]{2,1,0:T(8,128)S(1)} %get-tuple-element.27), channel_id=1, source_target_pairs={{1,2},{2,1},{3,4},{4,3},{5,6},{6,5},{7,8},{8,7},{9,10},{10,9},{11,... | collective-permute-start | bytes 786440 | tf_op jit(solution)/shard_map/ppermute | solution.py:36
  6.2 15.7 %collective-permute-start.2 = (f32[16,32,128]{2,1,0:T(8,128)S(1)}, f32[16,32,128]{2,1,0:T(8,128)S(1)}, u32[]{:S(2)}, u32[]{:S(2)}) collective-permute-start(f32[16,32,128]{2,1,0:T(8,128)S(1)} %get-tuple-element.28), channel_id=1, source_target_pairs={{0,32},{32,0},{64,96},{96,64},{128,160},{160,128},{192,224},{224,1... | collective-permute-start | bytes 786440 | tf_op jit(solution)/shard_map/ppermute | solution.py:36
  8.1 13.8 %collective-permute-start.3 = (f32[16,32,128]{2,1,0:T(8,128)S(1)}, f32[16,32,128]{2,1,0:T(8,128)S(1)}, u32[]{:S(2)}, u32[]{:S(2)}) collective-permute-start(f32[16,32,128]{2,1,0:T(8,128)S(1)} %get-tuple-element.29), channel_id=1, source_target_pairs={{32,64},{64,32},{96,128},{128,96},{160,192},{192,160},{33,65},{65,... | collective-permute-start | bytes 786440 | tf_op jit(solution)/shard_map/ppermute | solution.py:36
  15.2 10.5 %collective-permute-start.4 = (f32[5,32,128]{2,1,0:T(8,128)S(1)}, f32[5,32,128]{2,1,0:T(8,128)S(1)}, u32[]{:S(2)}, u32[]{:S(2)}) collective-permute-start(f32[5,32,128]{2,1,0:T(8,128)S(1)} %get-tuple-element.38), channel_id=1, source_target_pairs={{0,32},{32,0},{64,96},{96,64},{128,160},{160,128},{192,224},{224,1... | collective-permute-start | bytes 245768 | tf_op jit(solution)/shard_map/ppermute | solution.py:36
  17.1 8.6 %collective-permute-start.5 = (f32[5,32,128]{2,1,0:T(8,128)S(1)}, f32[5,32,128]{2,1,0:T(8,128)S(1)}, u32[]{:S(2)}, u32[]{:S(2)}) collective-permute-start(f32[5,32,128]{2,1,0:T(8,128)S(1)} %get-tuple-element.39), channel_id=1, source_target_pairs={{32,64},{64,32},{96,128},{128,96},{160,192},{192,160},{33,65},{65,... | collective-permute-start | bytes 245768 | tf_op jit(solution)/shard_map/ppermute | solution.py:36
